TPU v7x, 32 devices: a whole 2x2x4 slice. The times are simulated.
32 devices in a mesh: seq: 8 (over z, y), ch: 4 (over x, core).
Axes of the slice: x: 2, y: 2, z: 4, core: 2. Of those that a mesh axis runs over, the one named last changes fastest.
Arguments:
- query_input: bfloat16 [1024, 2048], P('seq', 'ch'), may hold values from -6 to 6
- key_input: bfloat16 [1024, 2048], P('seq', 'ch'), may hold values from -6 to 6
- value_input: bfloat16 [1024, 2048], P('seq', 'ch'), may hold values from -6 to 6
- cotangent: bfloat16 [1024, 2048], P('seq', 'ch'), may hold values from -6 to 6
- filter_taps: float32 [1024, 2048], P('seq', 'ch'), may hold values from -0.1875 to 0.1875
- skip_gain: float32 [2048], P('ch'), may hold values from -2 to 2
Outputs:
- output: bfloat16 [1024, 2048], P('seq', 'ch')
- query_grad: bfloat16 [1024, 2048], P('seq', 'ch')
- key_grad: bfloat16 [1024, 2048], P('seq', 'ch')
- value_grad: bfloat16 [1024, 2048], P('seq', 'ch')
- filter_grad: float32 [1024, 2048], P('seq', 'ch')
- skip_grad: float32 [2048], P('ch')
- grad_rms: float32 [], replicated
All inputs are finite; a program needn't handle non-finite values.
Results may differ from a plain program's by a relative error of at most 0.0014.
Values sent between devices are 32-bit elements; how exact they have to be, the bound alone decides.
A program may use at most 64 MiB of HBM per device.

v0:
```python
import math

import jax
import jax.numpy as jnp
from jax import lax
from jax.sharding import PartitionSpec as P


def complex_mul(left_op, right_op):
    return jnp.stack(
        [
            left_op[0] * right_op[0] - left_op[1] * right_op[1],
            left_op[0] * right_op[1] + left_op[1] * right_op[0],
        ]
    )


def conj_of(stacked):
    return jnp.stack([stacked[0], -stacked[1]])


def dft_table(length, direction):
    counter = jnp.arange(length)
    angles = (
        2.0 * math.pi / length * (counter[:, None] * counter[None, :] % length).astype(jnp.float32)
    )
    return (jnp.cos(angles), direction * jnp.sin(angles))


def dft_along(stacked, length, direction, pattern):
    table_re, table_im = dft_table(length, direction)

    def contract(table, part_in):
        return jnp.einsum(pattern, table, part_in, precision=lax.Precision.HIGHEST)

    real_out = contract(table_re, stacked[0]) - contract(table_im, stacked[1])
    imag_out = contract(table_re, stacked[1]) + contract(table_im, stacked[0])
    return jnp.stack([real_out, imag_out])


def grid_twiddle(devices, block, direction):
    seq_length = devices * block
    counter = jnp.arange(devices)[:, None] * jnp.arange(block)[None, :] % seq_length
    angles = direction * 2.0 * math.pi / seq_length * counter.astype(jnp.float32)
    return jnp.stack([jnp.cos(angles), jnp.sin(angles)])[:, None, None]


def local_forward(stacked, devices, block):
    array_shape = stacked.shape
    stacked = stacked.reshape(array_shape[0], array_shape[1], array_shape[2], devices, block)
    stacked = dft_along(stacked, devices, -1.0, "kj,scjp->sckp")
    stacked = complex_mul(stacked, grid_twiddle(devices, block, -1.0))
    return dft_along(stacked, block, -1.0, "kp,scjp->scjk")


def local_inverse(stacked, devices, block):
    stacked = dft_along(stacked, block, 1.0, "kp,scjp->scjk")
    stacked = complex_mul(stacked, grid_twiddle(devices, block, 1.0))
    stacked = dft_along(stacked, devices, 1.0, "kj,scjp->sckp")
    array_shape = stacked.shape
    return stacked.reshape(array_shape[0], array_shape[1], array_shape[2], devices * block) / (
        devices * block
    )


def modulated(signals, cosine, sine_part):
    zero_part = jnp.zeros_like(signals)
    return jnp.stack(
        [
            jnp.concatenate([signals, signals * cosine]),
            jnp.concatenate([zero_part, -signals * sine_part]),
        ]
    )


def spectral_products(spectrum):
    mixed_spec = spectrum[:, 0::3]
    gated_spec = spectrum[:, 1::3]
    taps_spec = spectrum[:, 2::3]
    out_spec = complex_mul(mixed_spec, taps_spec)
    back_spec = complex_mul(gated_spec, conj_of(taps_spec))
    grad_spec = complex_mul(gated_spec, conj_of(mixed_spec))
    return jnp.stack(
        [
            out_spec[:, 0],
            back_spec[:, 0],
            grad_spec[:, 0],
            out_spec[:, 1],
            back_spec[:, 1],
            grad_spec[:, 1],
        ],
        axis=1,
    )


def unfold(series, cosine, sine_part):
    return tuple(
        (
            0.5
            * (
                series[0, signal_index]
                + cosine * series[0, signal_index + 3]
                - sine_part * series[1, signal_index + 3]
            )
            for signal_index in range(3)
        )
    )


def channel_local(mixed_in, gated_cot, filter_taps, devices):
    pieces = (
        lax.all_to_all(mixed_in, "seq", split_axis=1, concat_axis=0, tiled=True),
        lax.all_to_all(gated_cot, "seq", split_axis=1, concat_axis=0, tiled=True),
        lax.all_to_all(filter_taps, "seq", split_axis=1, concat_axis=0, tiled=True),
    )
    laid = jnp.transpose(jnp.stack(pieces), (0, 2, 1))
    seq_length = laid.shape[2]
    block = seq_length // devices
    angles = math.pi / seq_length * jnp.arange(seq_length).astype(jnp.float32)
    cosine = jnp.cos(angles)
    sine_row = jnp.sin(angles)
    spectrum = local_forward(modulated(laid, cosine, sine_row), devices, block)
    series = local_inverse(spectral_products(spectrum), devices, block)
    results = unfold(series, cosine, sine_row)
    return (
        lax.all_to_all(results[0].T, "seq", split_axis=0, concat_axis=1, tiled=True),
        lax.all_to_all(results[1].T, "seq", split_axis=0, concat_axis=1, tiled=True),
        lax.all_to_all(results[2].T, "seq", split_axis=0, concat_axis=1, tiled=True),
    )


def body(query_input, key_input, value_input, cotangent, filter_taps, skip_gain):
    devices = lax.axis_size("seq")
    row_count, channels = query_input.shape
    seq_length = row_count * devices
    query_val = query_input.astype(jnp.float32)
    key_val = key_input.astype(jnp.float32)
    value_val = value_input.astype(jnp.float32)
    cot_val = cotangent.astype(jnp.float32)
    mixed_in = key_val * value_val
    gated_cot = query_val * cot_val
    conv_out, back_conv, kernel_grad = channel_local(mixed_in, gated_cot, filter_taps, devices)
    inner_sum = conv_out + skip_gain[None, :] * mixed_in
    mixed_grad = back_conv + skip_gain[None, :] * gated_cot
    output = (query_val * inner_sum).astype(jnp.bfloat16)
    query_grad = (cot_val * inner_sum).astype(jnp.bfloat16)
    key_grad = (mixed_grad * value_val).astype(jnp.bfloat16)
    value_grad = (mixed_grad * key_val).astype(jnp.bfloat16)
    time_scale = 1.0 / math.sqrt(seq_length)
    filter_grad = kernel_grad * time_scale
    filter_sq = jnp.sum(filter_grad * filter_grad)
    skip_part = jnp.sum(gated_cot * mixed_in, axis=0) * time_scale
    skip_grad = lax.psum(skip_part, "seq")
    total_sq = lax.psum(filter_sq + jnp.sum(skip_grad * skip_grad) / devices, ("seq", "ch"))
    grad_rms = jnp.sqrt(total_sq / (channels * lax.axis_size("ch") * (seq_length + 1)))
    return (output, query_grad, key_grad, value_grad, filter_grad, skip_grad, grad_rms)


def solution(mesh):
    return jax.shard_map(
        body,
        mesh=mesh,
        in_specs=(
            P("seq", "ch"),
            P("seq", "ch"),
            P("seq", "ch"),
            P("seq", "ch"),
            P("seq", "ch"),
            P("ch"),
        ),
        out_specs=(
            P("seq", "ch"),
            P("seq", "ch"),
            P("seq", "ch"),
            P("seq", "ch"),
            P("seq", "ch"),
            P("ch"),
            P(),
        ),
        check_vma=False,
    )
```

profile of v0, /device:TPU:0, one launch (start us, length us, event | category | flops | bytes accessed | tf_op | source)
XLA Modules:
  0.0 178.6 jit_solution(7563937218899946480)
XLA Ops:
  0.7 1.1 copy.46
  3.5 7.3 %all-to-all-start = ((f32[128,8,64]{0,2,1:T(8,128)}), f32[128,8,64]{0,2,1:T(8,128)S(1)}, u32[]{:S(2)}, u32[]{:S(2)}) async-start(f32[128,8,64]{0,2,1:T(8,128)} %bitcast), calls=%async_computation | async-start | bytes 524288 | tf_op jit(solution)/shard_map/all_to_all | solution.py:112
  11.8 7.9 %all-to-all-done = f32[128,8,64]{0,2,1:T(8,128)S(1)} async-done(((f32[128,8,64]{0,2,1:T(8,128)}), f32[128,8,64]{0,2,1:T(8,128)S(1)}, u32[]{:S(2)}, u32[]{:S(2)}) %all-to-all-start) | async-done | bytes 262176 | tf_op jit(solution)/shard_map/all_to_all | solution.py:112
  19.7 3.6 %all-to-all-start.1 = ((f32[128,8,64]{0,2,1:T(8,128)}), f32[128,8,64]{0,2,1:T(8,128)S(1)}, u32[]{:S(2)}, u32[]{:S(2)}) async-start(f32[128,8,64]{0,2,1:T(8,128)} %bitcast.2), calls=%async_computation.1 | async-start | bytes 524288 | tf_op jit(solution)/shard_map/all_to_all | solution.py:113
  24.2 7.7 %all-to-all-done.1 = f32[128,8,64]{0,2,1:T(8,128)S(1)} async-done(((f32[128,8,64]{0,2,1:T(8,128)}), f32[128,8,64]{0,2,1:T(8,128)S(1)}, u32[]{:S(2)}, u32[]{:S(2)}) %all-to-all-start.1) | async-done | bytes 262176 | tf_op jit(solution)/shard_map/all_to_all | solution.py:113
  31.9 3.6 %all-to-all-start.2 = ((f32[128,8,64]{0,2,1:T(8,128)}), f32[128,8,64]{0,2,1:T(8,128)S(1)}, u32[]{:S(2)}, u32[]{:S(2)}) async-start(f32[128,8,64]{0,2,1:T(8,128)} %bitcast.4), calls=%async_computation.2 | async-start | bytes 524288 | tf_op jit(solution)/shard_map/all_to_all | solution.py:114
  36.1 7.9 %all-to-all-done.2 = f32[128,8,64]{0,2,1:T(8,128)S(1)} async-done(((f32[128,8,64]{0,2,1:T(8,128)}), f32[128,8,64]{0,2,1:T(8,128)S(1)}, u32[]{:S(2)}, u32[]{:S(2)}) %all-to-all-start.2) | async-done | bytes 262176 | tf_op jit(solution)/shard_map/all_to_all | solution.py:114
  45.5 1.4 fusion.2
  46.9 1.4 fusion
  48.4 1.5 fusion.10
  49.9 1.5 fusion.13
  51.4 1.7 fusion.33
  53.1 1.7 fusion.29
  54.8 1.9 %subtract_bitcast_fusion.1 = f32[1,6,64,8,128]{4,3,2,1,0:T(8,128)S(1)} fusion(f32[6,64,8,128]{3,2,1,0:T(8,128)S(1)} %fusion.33, f32[6,64,128,8]{2,3,1,0:T(8,128)S(1)} %fusion.13, f32[6,64,128,8]{2,3,1,0:T(8,128)S(1)} %fusion.10, f32[8,128]{1,0:T(8,128)S(1)} %get-tuple-element.55, f32[8,128]{1,0:T(8,128)S(1)} %get-tuple-element.56), kind=kOutput, calls=%fused_computation.24 | convolution fusion | flops 605798400 | bytes 6299648 | tf_op jit(solution)/shard_map/kp,scjp->scjk/dot_general | solution.py:34
  56.7 1.7 add_bitcast_fusion.1
  59.5 1.7 fusion.16
  61.2 1.7 fusion.17
  62.9 1.7 convolution_subtract_fusion
  64.6 1.7 convolution_add_fusion
  66.3 1.8 %fusion.27 = f32[6,64,128,8]{2,3,1,0:T(8,128)S(1)} fusion(f32[6,64,8,128]{3,2,1,0:T(8,128)S(1)} %convolution_add_fusion, f32[6,64,8,128]{3,2,1,0:T(8,128)S(1)} %convolution_subtract_fusion, f32[8,128]{1,0:T(8,128)S(1)} %get-tuple-element.57, f32[8,128]{1,0:T(8,128)S(1)} %get-tuple-element.58), kind=kOutput, calls=%fused_computation.57 | convolution fusion | flops 38929280 | bytes 4726784 | tf_op jit(solution)/shard_map/kj,scjp->sckp/dot_general | solution.py:34
  68.1 2.7 %fusion.28 = f32[6,64,128,8]{2,3,1,0:T(8,128)} fusion(f32[6,64,8,128]{3,2,1,0:T(8,128)S(1)} %convolution_add_fusion, f32[6,64,8,128]{3,2,1,0:T(8,128)S(1)} %convolution_subtract_fusion, f32[8,128]{1,0:T(8,128)S(1)} %get-tuple-element.57, f32[8,128]{1,0:T(8,128)S(1)} %get-tuple-element.58), kind=kOutput, calls=%fused_computation.58 | convolution fusion | flops 38929280 | bytes 4726784 | tf_op jit(solution)/shard_map/kj,scjp->sckp/dot_general | solution.py:34
  70.8 2.8 %subtract_bitcast_fusion = f32[6,64,8,128]{3,2,1,0:T(8,128)} fusion(f32[6,64,128,8]{2,3,1,0:T(8,128)S(1)} %fusion.27, f32[6,64,8,128]{3,2,1,0:T(8,128)S(1)} %convolution_add_fusion, f32[6,64,8,128]{3,2,1,0:T(8,128)S(1)} %convolution_subtract_fusion, f32[8,128]{1,0:T(8,128)S(1)} %get-tuple-element.57, f32[8,128]{1,0:T(8,128)S(1)} %get-tuple-element.58), kind=kOutput, calls=%fused_computation.20 | convolution fusion | flops 39322496 | bytes 6299648 | tf_op jit(solution)/shard_map/kj,scjp->sckp/dot_general | solution.py:34
  73.6 2.6 %stack.68 = f32[1,6,64,1024]{3,2,1,0:T(8,128)} reshape(f32[6,64,8,128]{3,2,1,0:T(8,128)} %subtract_bitcast_fusion) | data formatting | bytes 3145728 | tf_op jit(solution)/shard_map/stack | solution.py:38
  76.2 4.1 %add_bitcast_fusion = f32[6,64,8,128]{3,2,1,0:T(8,128)} fusion(f32[6,64,128,8]{2,3,1,0:T(8,128)} %fusion.28, f32[6,64,8,128]{3,2,1,0:T(8,128)S(1)} %convolution_add_fusion, f32[6,64,8,128]{3,2,1,0:T(8,128)S(1)} %convolution_subtract_fusion, f32[8,128]{1,0:T(8,128)S(1)} %get-tuple-element.57, f32[8,128]{1,0:T(8,128)S(1)} %get-tuple-element.58), kind=kOutput, calls=%fused_computation.19 | convolution fusion | flops 39322496 | bytes 6299648 | tf_op jit(solution)/shard_map/kj,scjp->sckp/dot_general | solution.py:34
  80.3 1.6 stack.69
  83.5 3.6 %all-to-all-start.3 = ((f32[8,128,64]{1,2,0:T(8,128)}), f32[8,128,64]{1,2,0:T(8,128)S(1)}, u32[]{:S(2)}, u32[]{:S(2)}) async-start(f32[8,128,64]{1,2,0:T(8,128)} %bitcast.232), calls=%async_computation.3 | async-start | bytes 524288 | tf_op jit(solution)/shard_map/all_to_all | solution.py:126
  87.8 7.8 %all-to-all-done.3 = f32[8,128,64]{1,2,0:T(8,128)S(1)} async-done(((f32[8,128,64]{1,2,0:T(8,128)}), f32[8,128,64]{1,2,0:T(8,128)S(1)}, u32[]{:S(2)}, u32[]{:S(2)}) %all-to-all-start.3) | async-done | bytes 262176 | tf_op jit(solution)/shard_map/all_to_all | solution.py:126
  95.6 3.5 %all-to-all-start.4 = ((f32[8,128,64]{1,2,0:T(8,128)}), f32[8,128,64]{1,2,0:T(8,128)S(1)}, u32[]{:S(2)}, u32[]{:S(2)}) async-start(f32[8,128,64]{1,2,0:T(8,128)} %bitcast.231), calls=%async_computation.4 | async-start | bytes 524288 | tf_op jit(solution)/shard_map/all_to_all | solution.py:127
  99.9 7.8 %all-to-all-done.4 = f32[8,128,64]{1,2,0:T(8,128)S(1)} async-done(((f32[8,128,64]{1,2,0:T(8,128)}), f32[8,128,64]{1,2,0:T(8,128)S(1)}, u32[]{:S(2)}, u32[]{:S(2)}) %all-to-all-start.4) | async-done | bytes 262176 | tf_op jit(solution)/shard_map/all_to_all | solution.py:127
  107.7 3.6 %all-to-all-start.5 = ((f32[8,128,64]{1,2,0:T(8,128)}), f32[8,128,64]{1,2,0:T(8,128)S(1)}, u32[]{:S(2)}, u32[]{:S(2)}) async-start(f32[8,128,64]{1,2,0:T(8,128)} %bitcast.230), calls=%async_computation.5 | async-start | bytes 524288 | tf_op jit(solution)/shard_map/all_to_all | solution.py:128
  111.6 21.8 %psum.14 = f32[512]{0:T(512)S(1)} all-reduce(f32[512]{0:T(512)S(1)} %broadcast_multiply_fusion.2), channel_id=1, replica_groups=mesh['seq'=8,'ch'=4] {'seq'}, use_global_device_ids=true, to_apply=%region_1.2 | all-reduce | flops 512 | bytes 4096 | tf_op jit(solution)/shard_map/psum | solution.py:153
  136.0 36.8 %psum.15 = f32[]{:T(128)} all-reduce(f32[]{:T(128)S(6)} %add.158), channel_id=1, replica_groups=mesh['seq'=8,'ch'=4] {'seq','ch'}, use_global_device_ids=true, to_apply=%region_4.5 | all-reduce | flops 1 | bytes 8 | tf_op jit(solution)/shard_map/psum | solution.py:154
  (62 shorter events, 15.0 us)
Async XLA Ops:
  0.6 10.2 %copy-start.4 = (bf16[128,512]{1,0:T(8,128)(2,1)S(1)}, bf16[128,512]{1,0:T(8,128)(2,1)}, u32[]{:S(2)}) copy-start(bf16[128,512]{1,0:T(8,128)(2,1)} %param.6) | copy-start | bytes 393220
  0.6 10.3 %copy-start.5 = (bf16[128,512]{1,0:T(8,128)(2,1)S(1)}, bf16[128,512]{1,0:T(8,128)(2,1)}, u32[]{:S(2)}) copy-start(bf16[128,512]{1,0:T(8,128)(2,1)} %param.9) | copy-start | bytes 393220
  0.7 22.7 %copy-start.3 = (f32[128,512]{1,0:T(8,128)S(1)}, f32[128,512]{1,0:T(8,128)}, u32[]{:S(2)}) copy-start(f32[128,512]{1,0:T(8,128)} %param.10) | copy-start | bytes 786436
  3.5 16.2 %all-to-all-start = ((f32[128,8,64]{0,2,1:T(8,128)}), f32[128,8,64]{0,2,1:T(8,128)S(1)}, u32[]{:S(2)}, u32[]{:S(2)}) async-start(f32[128,8,64]{0,2,1:T(8,128)} %bitcast), calls=%async_computation | async-start | bytes 524288 | tf_op jit(solution)/shard_map/all_to_all | solution.py:112
  11.1 24.6 %copy-start.1 = (bf16[128,512]{0,1:T(8,128)(2,1)}, bf16[128,512]{0,1:T(8,128)(2,1)S(1)}, u32[]{:S(2)}) copy-start(bf16[128,512]{0,1:T(8,128)(2,1)S(1)} %copy.49) | copy-start | bytes 393220
  19.7 12.2 %all-to-all-start.1 = ((f32[128,8,64]{0,2,1:T(8,128)}), f32[128,8,64]{0,2,1:T(8,128)S(1)}, u32[]{:S(2)}, u32[]{:S(2)}) async-start(f32[128,8,64]{0,2,1:T(8,128)} %bitcast.2), calls=%async_computation.1 | async-start | bytes 524288 | tf_op jit(solution)/shard_map/all_to_all | solution.py:113
  31.9 12.1 %all-to-all-start.2 = ((f32[128,8,64]{0,2,1:T(8,128)}), f32[128,8,64]{0,2,1:T(8,128)S(1)}, u32[]{:S(2)}, u32[]{:S(2)}) async-start(f32[128,8,64]{0,2,1:T(8,128)} %bitcast.4), calls=%async_computation.2 | async-start | bytes 524288 | tf_op jit(solution)/shard_map/all_to_all | solution.py:114
  80.3 1.9 %copy-start = (f32[1,6,64,1024]{3,2,1,0:T(8,128)S(1)}, f32[1,6,64,1024]{3,2,1,0:T(8,128)}, u32[]{:S(2)}) copy-start(f32[1,6,64,1024]{3,2,1,0:T(8,128)} %stack.68) | copy-start | bytes 4718596
  82.8 28.5 %copy-start.2 = (bf16[128,512]{0,1:T(8,128)(2,1)S(1)}, bf16[128,512]{0,1:T(8,128)(2,1)}, u32[]{:S(2)}) copy-start(bf16[128,512]{0,1:T(8,128)(2,1)} %copy-done.1) | copy-start | bytes 393220
  82.8 28.5 %copy-start.7 = (f32[512]{0:T(512)S(1)}, f32[512]{0:T(512)}, u32[]{:S(2)}) copy-start(f32[512]{0:T(512)} %param.11) | copy-start | bytes 6148
  83.5 12.1 %all-to-all-start.3 = ((f32[8,128,64]{1,2,0:T(8,128)}), f32[8,128,64]{1,2,0:T(8,128)S(1)}, u32[]{:S(2)}, u32[]{:S(2)}) async-start(f32[8,128,64]{1,2,0:T(8,128)} %bitcast.232), calls=%async_computation.3 | async-start | bytes 524288 | tf_op jit(solution)/shard_map/all_to_all | solution.py:126
  95.6 12.1 %all-to-all-start.4 = ((f32[8,128,64]{1,2,0:T(8,128)}), f32[8,128,64]{1,2,0:T(8,128)S(1)}, u32[]{:S(2)}, u32[]{:S(2)}) async-start(f32[8,128,64]{1,2,0:T(8,128)} %bitcast.231), calls=%async_computation.4 | async-start | bytes 524288 | tf_op jit(solution)/shard_map/all_to_all | solution.py:127
  107.7 27.0 %all-to-all-start.5 = ((f32[8,128,64]{1,2,0:T(8,128)}), f32[8,128,64]{1,2,0:T(8,128)S(1)}, u32[]{:S(2)}, u32[]{:S(2)}) async-start(f32[8,128,64]{1,2,0:T(8,128)} %bitcast.230), calls=%async_computation.5 | async-start | bytes 524288 | tf_op jit(solution)/shard_map/all_to_all | solution.py:128
  133.4 44.0 %copy-start.6 = (f32[512]{0:T(512)}, f32[512]{0:T(512)S(1)}, u32[]{:S(2)}) copy-start(f32[512]{0:T(512)S(1)} %psum.14) | copy-start | bytes 6148
where the time goes:
time: 180 us; the launch traced here: 179 us
  blocking collectives  58.7 us (33%)
  waiting for transfers between devices  39.2 us (22%)
  matrix products  31.1 us (17%)
  starting transfers between devices  25.1 us (14%)
  local copies, waits for them, and re-layouts  15.4 us (9%)
  other arithmetic  4.91 us (3%)
  between operations  4.19 us (2%)
    psum x1, blocking collectives, body(): lax.psum(filter_sq + jnp.sum(skip_grad * skip_grad) / devices, ('seq', 'c...  36.8 us
    dot_general x16, matrix products, contract(): return jnp.einsum(pattern, table, part_in, precision=lax.Precision.HIGHEST)  31.1 us
    psum x1, blocking collectives, body(): skip_grad = lax.psum(skip_part, 'seq')  21.8 us
    unnamed x28, local copies, waits for them, and re-layouts  8.03 us
    all_to_all x1, waiting for transfers between devices, channel_local(): lax.all_to_all(filter_taps, 'seq', split_axis=1, concat_axis=0, tiled=True)  7.93 us
    all_to_all x1, waiting for transfers between devices, channel_local(): lax.all_to_all(mixed_in, 'seq', split_axis=1, concat_axis=0, tiled=True)  7.91 us
    all_to_all x1, waiting for transfers between devices, channel_local(): lax.all_to_all(results[0].T, 'seq', split_axis=0, concat_axis=1, tiled=True)  7.81 us
    all_to_all x1, waiting for transfers between devices, channel_local(): lax.all_to_all(results[1].T, 'seq', split_axis=0, concat_axis=1, tiled=True)  7.81 us
  transfers between devices with their start and end apart: 6, of which 5 were waited for; matrix products, arithmetic and copies ran while one was open for 3% of the time, Pallas kernels for 0%

commit v1 on v0

--- a/solution.py
+++ b/solution.py
@@ -1,9 +1,16 @@
+import functools
 import math
 
 import jax
 import jax.numpy as jnp
+import numpy as np
 from jax import lax
+from jax.experimental import pallas as pl
+from jax.experimental.pallas import tpu as pltpu
 from jax.sharding import PartitionSpec as P
+
+LANES = 128
+MESH = pl.DeviceIdType.MESH
 
 
 def complex_mul(left_op, right_op):
@@ -156,9 +163,349 @@
     return (output, query_grad, key_grad, value_grad, filter_grad, skip_grad, grad_rms)
 
 
+def split_high_low(array):
+    high = array.astype(jnp.bfloat16)
+    return high, (array - high.astype(jnp.float32)).astype(jnp.bfloat16)
+
+
+def half_tables(points):
+    odd = 2 * np.arange(points, dtype=np.int64) + 1
+    angles = math.pi / (4 * points) * (odd[:, None] * odd[None, :] % (8 * points))
+    parts = []
+    for table in (np.cos(angles), np.sin(angles)):
+        table = table.astype(np.float32)
+        high = table.astype(jnp.bfloat16)
+        parts += [high, (table - high.astype(np.float32)).astype(jnp.bfloat16)]
+    shift = math.pi / (4 * points) * odd[:, None] * np.ones((1, LANES))
+    return np.stack(parts), np.stack([np.cos(shift), np.sin(shift)]).astype(np.float32)
+
+
+def kernel(
+    devices, groups, count,
+    q_ref, k_ref, v_ref, c_ref, h_ref, skip_ref, table_hbm, twist_hbm,
+    out_ref, dq_ref, dk_ref, dv_ref, dh_ref, dskip_ref, rms_ref,
+    x_buf, g_buf, wide, send, recv, spec, prod, back, home, tail, tail_home, sq_send, sq_recv,
+    table, twist, send_sem, recv_sem, own_sem, tail_send, tail_recv, sq_ssem, sq_rsem, load_sem,
+):
+    me = lax.axis_index("seq")
+    mine = lax.axis_index("ch")
+    rows, channels = q_ref.shape
+    half = rows // 2
+    points = half * devices
+    low = LANES // 2
+    time_scale = 1.0 / math.sqrt(2 * points)
+
+    barrier = pltpu.get_barrier_semaphore()
+    for k in range(1, devices):
+        pl.semaphore_signal(
+            barrier, inc=1, device_id={"seq": lax.rem(me + k, devices)}, device_id_type=MESH
+        )
+    for k in range(1, groups):
+        pl.semaphore_signal(
+            barrier, inc=1, device_id={"ch": lax.rem(mine + k, groups)}, device_id_type=MESH
+        )
+    loads = (
+        pltpu.make_async_copy(table_hbm, table, load_sem.at[0]),
+        pltpu.make_async_copy(twist_hbm, twist, load_sem.at[1]),
+    )
+    for load in loads:
+        load.start()
+
+    def remote(source, target, slot, k):
+        peer = lax.rem(me + k, devices)
+        return pltpu.make_async_remote_copy(
+            src_ref=source.at[peer],
+            dst_ref=target.at[me],
+            send_sem=send_sem.at[slot, k],
+            recv_sem=recv_sem.at[slot, k],
+            device_id={"seq": peer},
+            device_id_type=MESH,
+        )
+
+    def own(source, target, slot):
+        return pltpu.make_async_copy(source.at[me], target.at[me], own_sem.at[slot])
+
+    def tail_copy(k):
+        peer = lax.rem(me + k, devices)
+        return pltpu.make_async_remote_copy(
+            src_ref=tail,
+            dst_ref=tail_home.at[me],
+            send_sem=tail_send.at[k],
+            recv_sem=tail_recv.at[k],
+            device_id={"seq": peer},
+            device_id_type=MESH,
+        )
+
+    def square_copy(k):
+        peer = lax.rem(mine + k, groups)
+        return pltpu.make_async_remote_copy(
+            src_ref=sq_send,
+            dst_ref=sq_recv.at[mine],
+            send_sem=sq_ssem.at[k],
+            recv_sem=sq_rsem.at[k],
+            device_id={"ch": peer},
+            device_id_type=MESH,
+        )
+
+    def start_all(source, target, slot):
+        for k in range(1, devices):
+            remote(source, target, slot, k).start()
+        own(source, target, slot).start()
+
+    def wait_arrivals(source, target, slot):
+        for k in range(1, devices):
+            remote(source, target, slot, k).wait_recv()
+        own(source, target, slot).wait()
+
+    first = lax.broadcasted_iota(jnp.int32, (half, LANES), 1) < low
+
+    def pack(source, signal):
+        for j in range(channels // LANES):
+            even = source[j, pl.ds(0, half, stride=2), :]
+            odd = source[j, pl.ds(1, half, stride=2), :]
+            send[signal, 2 * j] = jnp.where(first, even, pltpu.roll(odd, low, 1))
+            send[signal, 2 * j + 1] = jnp.where(first, pltpu.roll(even, low, 1), odd)
+
+    def unpack(signal):
+        for j in range(channels // LANES):
+            left = home[signal, 2 * j]
+            right = home[signal, 2 * j + 1]
+            wide[j, pl.ds(0, half, stride=2), :] = jnp.where(
+                first, left, pltpu.roll(right, low, 1)
+            )
+            wide[j, pl.ds(1, half, stride=2), :] = jnp.where(
+                first, pltpu.roll(left, low, 1), right
+            )
+
+    def columns_of(j):
+        return pl.ds(j * LANES, LANES)
+
+    blocks = channels // LANES
+    for j in range(blocks):
+        at = columns_of(j)
+        x_buf[j] = k_ref[:, at].astype(jnp.float32) * v_ref[:, at].astype(jnp.float32)
+    pack(x_buf, 0)
+    pl.semaphore_wait(barrier, devices + groups - 2)
+    start_all(send.at[0], recv.at[0], 0)
+    for j in range(blocks):
+        at = columns_of(j)
+        g_buf[j] = q_ref[:, at].astype(jnp.float32) * c_ref[:, at].astype(jnp.float32)
+    pack(g_buf, 1)
+    start_all(send.at[1], recv.at[1], 1)
+    for j in range(blocks):
+        wide[j] = h_ref[:, columns_of(j)]
+    pack(wide, 2)
+    start_all(send.at[2], recv.at[2], 2)
+    for load in loads:
+        load.wait()
+
+    def times(which, high, rest):
+        both = jnp.concatenate([high, rest], axis=1)
+        main = jnp.dot(table[2 * which], both, preferred_element_type=jnp.float32)
+        small = jnp.dot(table[2 * which + 1], high, preferred_element_type=jnp.float32)
+        return main[:, :LANES] + (main[:, LANES:] + small)
+
+    def forward(signal):
+        high, rest = split_high_low(recv[signal].reshape(points, LANES))
+        spec[signal, 0] = times(0, high, rest)
+        spec[signal, 1] = -times(1, high, rest)
+
+    def inverse(slot, scale):
+        real_high, real_rest = split_high_low(prod[0])
+        imag_high, imag_rest = split_high_low(prod[1])
+        series = times(0, real_high, real_rest) - times(1, imag_high, imag_rest)
+        series = series * (scale / points)
+        back[slot] = series.reshape(devices, half, LANES)
+        return series
+
+    step = 32
+
+    def halves(ref_row, part, at):
+        value = spec[ref_row, part, at, :]
+        turned = pltpu.roll(value, low, 1)
+        left = lax.broadcasted_iota(jnp.int32, (step, LANES), 1) < low
+        return value, turned, jnp.where(left, value, turned), jnp.where(left, turned, value)
+
+    def products(signal, other, conjugate):
+        sign = jnp.where(lax.broadcasted_iota(jnp.int32, (step, LANES), 1) < low, 1.0, -1.0)
+
+        @pl.loop(0, points // step)
+        def _(index):
+            at = pl.ds(pl.multiple_of(index * step, step), step)
+            cosine = twist[0, at, :]
+            sine = twist[1, at, :]
+            signed = sine * sign
+            _, _, even_re, odd_re = halves(other, 0, at)
+            _, _, even_im, odd_im = halves(other, 1, at)
+            a_re, as_re, _, _ = halves(signal, 0, at)
+            a_im, as_im, _, _ = halves(signal, 1, at)
+            p_re = even_re * cosine - even_im * sine
+            p_im = even_im * cosine + even_re * sine
+            if conjugate:
+                r_re = odd_re * cosine - odd_im * signed
+                r_im = odd_im * cosine + odd_re * signed
+                prod[0, at, :] = a_re * p_re + a_im * p_im + (as_re * r_re + as_im * r_im)
+                prod[1, at, :] = a_im * p_re - a_re * p_im + (as_im * r_re - as_re * r_im)
+            else:
+                r_re = odd_re * cosine + odd_im * signed
+                r_im = odd_im * cosine - odd_re * signed
+                prod[0, at, :] = a_re * p_re - a_im * p_im + (as_re * r_re - as_im * r_im)
+                prod[1, at, :] = a_im * p_re + a_re * p_im + (as_im * r_re + as_re * r_im)
+
+    wait_arrivals(send.at[0], recv.at[0], 0)
+    forward(0)
+    wait_arrivals(send.at[1], recv.at[1], 1)
+    forward(1)
+    products(1, 0, True)
+    series = inverse(0, time_scale)
+    start_all(back.at[0], home.at[0], 3)
+    direct = jnp.sum(
+        (recv[0] * recv[1]).reshape(points // 8, 8, LANES), axis=0
+    )
+    direct = jnp.sum(direct, axis=0, keepdims=True)
+    direct = jnp.broadcast_to(direct, (8, LANES)) * time_scale
+    direct = direct + pltpu.roll(direct, low, 1)
+    squares = jnp.sum((series * series).reshape(points // 8, 8, LANES), axis=0)
+    squares = squares + direct * direct * (1.0 / 16.0)
+    sq_send[...] = squares
+    for k in range(1, groups):
+        square_copy(k).start()
+    sq_own = pltpu.make_async_copy(sq_send, sq_recv.at[mine], load_sem.at[2])
+    sq_own.start()
+
+    wait_arrivals(send.at[2], recv.at[2], 2)
+    forward(2)
+    products(0, 2, False)
+    inverse(1, 1.0)
+    start_all(back.at[1], home.at[1], 4)
+    for k in range(1, groups):
+        square_copy(k).wait_recv()
+    sq_own.wait()
+    total = sq_recv[0]
+    for k in range(1, groups):
+        total = total + sq_recv[k]
+    tail[0] = direct
+    tail[1] = total
+    for k in range(1, devices):
+        tail_copy(k).start()
+    tail_own = pltpu.make_async_copy(tail, tail_home.at[me], load_sem.at[3])
+    tail_own.start()
+    products(1, 2, True)
+    inverse(2, 1.0)
+    start_all(back.at[2], home.at[2], 5)
+
+    wait_arrivals(back.at[0], home.at[0], 3)
+    unpack(0)
+    for j in range(blocks):
+        dh_ref[:, columns_of(j)] = wide[j]
+
+    wait_arrivals(back.at[1], home.at[1], 4)
+    unpack(1)
+    for j in range(blocks):
+        at = columns_of(j)
+        inner = wide[j] + skip_ref[:, at] * x_buf[j]
+        out_ref[:, at] = (q_ref[:, at].astype(jnp.float32) * inner).astype(jnp.bfloat16)
+        dq_ref[:, at] = (c_ref[:, at].astype(jnp.float32) * inner).astype(jnp.bfloat16)
+
+    for k in range(1, devices):
+        tail_copy(k).wait_recv()
+    tail_own.wait()
+    total = tail_home[0, 1]
+    for k in range(1, devices):
+        total = total + tail_home[k, 1]
+    total = jnp.sum(jnp.sum(total, axis=0, keepdims=True), axis=1, keepdims=True)
+    rms_ref[...] = jnp.sqrt(total / count)
+    for j in range(blocks):
+        left = lax.broadcasted_iota(jnp.int32, (8, LANES), 1) < low
+        both = jnp.where(left, tail_home[2 * j, 0], tail_home[2 * j + 1, 0])
+        dskip_ref[:, columns_of(j)] = both[0:1]
+
+    wait_arrivals(back.at[2], home.at[2], 5)
+    unpack(2)
+    for j in range(blocks):
+        at = columns_of(j)
+        grad = wide[j] + skip_ref[:, at] * g_buf[j]
+        dk_ref[:, at] = (v_ref[:, at].astype(jnp.float32) * grad).astype(jnp.bfloat16)
+        dv_ref[:, at] = (k_ref[:, at].astype(jnp.float32) * grad).astype(jnp.bfloat16)
+
+    for k in range(1, devices):
+        for slot in range(3):
+            remote(send.at[slot], recv.at[slot], slot, k).wait_send()
+            remote(back.at[slot], home.at[slot], slot + 3, k).wait_send()
+        tail_copy(k).wait_send()
+    for k in range(1, groups):
+        square_copy(k).wait_send()
+
+
+def fused_body(query_input, key_input, value_input, cotangent, filter_taps, skip_gain):
+    devices = lax.axis_size("seq")
+    groups = lax.axis_size("ch")
+    rows, channels = query_input.shape
+    half = rows // 2
+    points = half * devices
+    tables, twists = half_tables(points)
+    count = float(channels * groups * (rows * devices + 1))
+    vmem = pl.BlockSpec(memory_space=pltpu.VMEM)
+    hbm = pl.BlockSpec(memory_space=pl.ANY)
+    narrow = jax.ShapeDtypeStruct((rows, channels), jnp.bfloat16)
+    moved = (3, devices, half, LANES)
+    results = pl.pallas_call(
+        functools.partial(kernel, devices, groups, count),
+        out_shape=(
+            narrow,
+            narrow,
+            narrow,
+            narrow,
+            jax.ShapeDtypeStruct((rows, channels), jnp.float32),
+            jax.ShapeDtypeStruct((1, channels), jnp.float32),
+            jax.ShapeDtypeStruct((1, 1), jnp.float32),
+        ),
+        in_specs=[vmem] * 6 + [hbm] * 2,
+        out_specs=(vmem,) * 7,
+        scratch_shapes=[
+            pltpu.VMEM((channels // LANES, rows, LANES), jnp.float32),
+            pltpu.VMEM((channels // LANES, rows, LANES), jnp.float32),
+            pltpu.VMEM((channels // LANES, rows, LANES), jnp.float32),
+            pltpu.VMEM(moved, jnp.float32),
+            pltpu.VMEM(moved, jnp.float32),
+            pltpu.VMEM((3, 2, points, LANES), jnp.float32),
+            pltpu.VMEM((2, points, LANES), jnp.float32),
+            pltpu.VMEM(moved, jnp.float32),
+            pltpu.VMEM(moved, jnp.float32),
+            pltpu.VMEM((2, 8, LANES), jnp.float32),
+            pltpu.VMEM((devices, 2, 8, LANES), jnp.float32),
+            pltpu.VMEM((8, LANES), jnp.float32),
+            pltpu.VMEM((groups, 8, LANES), jnp.float32),
+            pltpu.VMEM(tables.shape, jnp.bfloat16),
+            pltpu.VMEM(twists.shape, jnp.float32),
+            pltpu.SemaphoreType.DMA((6, devices)),
+            pltpu.SemaphoreType.DMA((6, devices)),
+            pltpu.SemaphoreType.DMA((6,)),
+            pltpu.SemaphoreType.DMA((devices,)),
+            pltpu.SemaphoreType.DMA((devices,)),
+            pltpu.SemaphoreType.DMA((groups,)),
+            pltpu.SemaphoreType.DMA((groups,)),
+            pltpu.SemaphoreType.DMA((4,)),
+        ],
+        compiler_params=pltpu.CompilerParams(collective_id=0, has_side_effects=True),
+    )(
+        query_input, key_input, value_input, cotangent, filter_taps,
+        skip_gain.reshape(1, channels), jnp.asarray(tables), jnp.asarray(twists),
+    )
+    return (*results[:5], results[5].reshape(channels), results[6].reshape(()))
+
+
+def pick_body(query_input, *others):
+    devices = lax.axis_size("seq")
+    rows, channels = query_input.shape
+    fits = 2 * channels == LANES * devices and channels % LANES == 0 and rows % 16 == 0
+    chosen = fused_body if fits and rows * devices <= 2048 else body
+    return chosen(query_input, *others)
+
+
 def solution(mesh):
     return jax.shard_map(
-        body,
+        pick_body,
         mesh=mesh,
         in_specs=(
             P("seq", "ch"),

time: 180 us -> 57.6 us (0.32)
  blocking collectives: 58.7 us -> 0 us
  Pallas kernels: 0 us -> 45.7 us
  waiting for transfers between devices: 39.2 us -> 0 us
  matrix products: 31.1 us -> 0 us
  starting transfers between devices: 25.1 us -> 0 us
  local copies, waits for them, and re-layouts: 15.4 us -> 9.19 us
  other arithmetic: 4.91 us -> 0 us
    psum x2 -> x0, blocking collectives: 58.7 us -> none  [the longest x1 36.8 us: body(): lax.psum(filter_sq + jnp.sum(skip_grad * skip_grad) / devices, ('seq', 'c...]
    pallas_call x0 -> x1, Pallas kernels: none -> 45.7 us  [fused_body(): pl.pallas_call(functools.partial(kernel, devices, groups, count), out_sha...]
    all_to_all x6 -> x0, waiting for transfers between devices: 39.2 us -> none  [the longest x1 7.93 us: channel_local(): lax.all_to_all(filter_taps, 'seq', split_axis=1, concat_axis=0, tiled=True)]
    dot_general x16 -> x0, matrix products: 31.1 us -> none  [contract(): return jnp.einsum(pattern, table, part_in, precision=lax.Precision.HIGHEST)]
    all_to_all x6 -> x0, starting transfers between devices: 25.1 us -> none  [the longest x1 7.31 us: channel_local(): lax.all_to_all(mixed_in, 'seq', split_axis=1, concat_axis=0, tiled=True)]
    another operation x5 -> x0, local copies, waits for them, and re-layouts: 4.32 us -> none  [the longest x2 4.18 us: dft_along(): return jnp.stack([real_out, imag_out])]
    all_to_all x6 -> x0, local copies, waits for them, and re-layouts: 2.63 us -> none  [the longest x1 0.72 us: channel_local(): lax.all_to_all(results[0].T, 'seq', split_axis=0, concat_axis=1, tiled=True)]
    unnamed x28 -> x6, local copies, waits for them, and re-layouts: 8.03 us -> 9.19 us
  transfers between devices with their start and end apart: 6 -> 0, of which waited for: 5 -> 0; matrix products, arithmetic and copies ran while one was open for 3% -> 0% of each run, Pallas kernels for 0% -> 0%
where the time goes in v1:
time: 57.6 us; the launch traced here: 57.3 us
  Pallas kernels  45.7 us (79%)
  local copies, waits for them, and re-layouts  9.19 us (16%)
  between operations  2.41 us (4%)
    pallas_call x1, Pallas kernels, fused_body(): pl.pallas_call(functools.partial(kernel, devices, groups, count), out_sha...  45.7 us
    unnamed x6, local copies, waits for them, and re-layouts  9.19 us

profile of v1, /device:TPU:0, one launch (start us, length us, event | category | flops | bytes accessed | tf_op | source)
XLA Modules:
  0.0 57.3 jit_solution(12216315521192567713)
XLA Ops:
  0.6 45.7 %shard_map.135 = (bf16[128,512]{1,0:T(8,128)(2,1)}, bf16[128,512]{1,0:T(8,128)(2,1)}, bf16[128,512]{1,0:T(8,128)(2,1)}, bf16[128,512]{1,0:T(8,128)(2,1)}, f32[12...) custom-call(bf16[128,512]{1,0:T(8,128)(2,1)} %q_ref.1, bf16[128,512]{1,0:T(8,128)(2,1)} %k_ref.1, ...), custom_call_target="tpu_custom_call" | custom-call | tf_op jit(solution)/shard_map/pallas_call | solution.py:452
  46.3 1.6 %copy.22 = bf16[128,512]{1,0:T(8,128)(2,1)} copy(bf16[128,512]{1,0:T(8,128)(2,1)} %get-tuple-element.28) | data formatting | bytes 262144
  47.9 1.6 %copy.23 = bf16[128,512]{1,0:T(8,128)(2,1)} copy(bf16[128,512]{1,0:T(8,128)(2,1)} %get-tuple-element.29) | data formatting | bytes 262144
  49.5 1.6 %copy.24 = bf16[128,512]{1,0:T(8,128)(2,1)} copy(bf16[128,512]{1,0:T(8,128)(2,1)} %get-tuple-element.30) | data formatting | bytes 262144
  51.1 1.6 %copy.25 = bf16[128,512]{1,0:T(8,128)(2,1)} copy(bf16[128,512]{1,0:T(8,128)(2,1)} %get-tuple-element.31) | data formatting | bytes 262144
  52.6 1.7 %copy.26 = f32[128,512]{1,0:T(8,128)} copy(f32[128,512]{1,0:T(8,128)} %get-tuple-element.32) | data formatting | bytes 524288
  54.3 1.3 %copy.27 = f32[512]{0:T(512)} copy(f32[512]{0:T(512)} %bitcast.4) | data formatting | bytes 4096

commit v2 on v1

--- a/solution.py
+++ b/solution.py
@@ -182,8 +182,8 @@
 
 def kernel(
     devices, groups, count,
-    q_ref, k_ref, v_ref, c_ref, h_ref, skip_ref, table_hbm, twist_hbm,
-    out_ref, dq_ref, dk_ref, dv_ref, dh_ref, dskip_ref, rms_ref,
+    q_ref, k_ref, v_ref, c_ref, h_ref, table_hbm, twist_hbm,
+    flat, dskip_ref, rms_ref,
     x_buf, g_buf, wide, send, recv, spec, prod, back, home, tail, tail_home, sq_send, sq_recv,
     table, twist, send_sem, recv_sem, own_sem, tail_send, tail_recv, sq_ssem, sq_rsem, load_sem,
 ):
@@ -270,10 +270,10 @@
         for j in range(channels // LANES):
             left = home[signal, 2 * j]
             right = home[signal, 2 * j + 1]
-            wide[j, pl.ds(0, half, stride=2), :] = jnp.where(
+            flat[signal, j, pl.ds(0, half, stride=2), :] = jnp.where(
                 first, left, pltpu.roll(right, low, 1)
             )
-            wide[j, pl.ds(1, half, stride=2), :] = jnp.where(
+            flat[signal, j, pl.ds(1, half, stride=2), :] = jnp.where(
                 first, pltpu.roll(left, low, 1), right
             )
 
@@ -396,16 +396,9 @@
 
     wait_arrivals(back.at[0], home.at[0], 3)
     unpack(0)
-    for j in range(blocks):
-        dh_ref[:, columns_of(j)] = wide[j]
 
     wait_arrivals(back.at[1], home.at[1], 4)
     unpack(1)
-    for j in range(blocks):
-        at = columns_of(j)
-        inner = wide[j] + skip_ref[:, at] * x_buf[j]
-        out_ref[:, at] = (q_ref[:, at].astype(jnp.float32) * inner).astype(jnp.bfloat16)
-        dq_ref[:, at] = (c_ref[:, at].astype(jnp.float32) * inner).astype(jnp.bfloat16)
 
     for k in range(1, devices):
         tail_copy(k).wait_recv()
@@ -414,7 +407,7 @@
     for k in range(1, devices):
         total = total + tail_home[k, 1]
     total = jnp.sum(jnp.sum(total, axis=0, keepdims=True), axis=1, keepdims=True)
-    rms_ref[...] = jnp.sqrt(total / count)
+    rms_ref[...] = total / count
     for j in range(blocks):
         left = lax.broadcasted_iota(jnp.int32, (8, LANES), 1) < low
         both = jnp.where(left, tail_home[2 * j, 0], tail_home[2 * j + 1, 0])
@@ -422,11 +415,6 @@
 
     wait_arrivals(back.at[2], home.at[2], 5)
     unpack(2)
-    for j in range(blocks):
-        at = columns_of(j)
-        grad = wide[j] + skip_ref[:, at] * g_buf[j]
-        dk_ref[:, at] = (v_ref[:, at].astype(jnp.float32) * grad).astype(jnp.bfloat16)
-        dv_ref[:, at] = (k_ref[:, at].astype(jnp.float32) * grad).astype(jnp.bfloat16)
 
     for k in range(1, devices):
         for slot in range(3):
@@ -435,6 +423,26 @@
         tail_copy(k).wait_send()
     for k in range(1, groups):
         square_copy(k).wait_send()
+
+
+def gate(
+    q_ref, k_ref, v_ref, c_ref, skip_ref, flat, direct_ref, mean_ref,
+    out_ref, dq_ref, dk_ref, dv_ref, dh_ref, dskip_ref, rms_ref,
+):
+    query_val = q_ref[...].astype(jnp.float32)
+    key_val = k_ref[...].astype(jnp.float32)
+    value_val = v_ref[...].astype(jnp.float32)
+    cot_val = c_ref[...].astype(jnp.float32)
+    skip = skip_ref[...]
+    inner = flat[1, 0] + skip * (key_val * value_val)
+    grad = flat[2, 0] + skip * (query_val * cot_val)
+    out_ref[...] = (query_val * inner).astype(jnp.bfloat16)
+    dq_ref[...] = (cot_val * inner).astype(jnp.bfloat16)
+    dk_ref[...] = (grad * value_val).astype(jnp.bfloat16)
+    dv_ref[...] = (grad * key_val).astype(jnp.bfloat16)
+    dh_ref[...] = flat[0, 0]
+    dskip_ref[...] = direct_ref[...]
+    rms_ref[...] = jnp.sqrt(mean_ref[...])
 
 
 def fused_body(query_input, key_input, value_input, cotangent, filter_taps, skip_gain):
@@ -449,19 +457,16 @@
     hbm = pl.BlockSpec(memory_space=pl.ANY)
     narrow = jax.ShapeDtypeStruct((rows, channels), jnp.bfloat16)
     moved = (3, devices, half, LANES)
-    results = pl.pallas_call(
+    blocks = channels // LANES
+    flat, direct, rms = pl.pallas_call(
         functools.partial(kernel, devices, groups, count),
         out_shape=(
-            narrow,
-            narrow,
-            narrow,
-            narrow,
-            jax.ShapeDtypeStruct((rows, channels), jnp.float32),
+            jax.ShapeDtypeStruct((3, blocks, rows, LANES), jnp.float32),
             jax.ShapeDtypeStruct((1, channels), jnp.float32),
             jax.ShapeDtypeStruct((1, 1), jnp.float32),
         ),
-        in_specs=[vmem] * 6 + [hbm] * 2,
-        out_specs=(vmem,) * 7,
+        in_specs=[vmem] * 5 + [hbm] * 2,
+        out_specs=(vmem,) * 3,
         scratch_shapes=[
             pltpu.VMEM((channels // LANES, rows, LANES), jnp.float32),
             pltpu.VMEM((channels // LANES, rows, LANES), jnp.float32),
@@ -489,8 +494,29 @@
         ],
         compiler_params=pltpu.CompilerParams(collective_id=0, has_side_effects=True),
     )(
-        query_input, key_input, value_input, cotangent, filter_taps,
-        skip_gain.reshape(1, channels), jnp.asarray(tables), jnp.asarray(twists),
+        query_input, key_input, value_input, cotangent, filter_taps, jnp.asarray(tables), jnp.asarray(twists),
+    )
+    column = pl.BlockSpec((rows, LANES), lambda j: (0, j))
+    line = pl.BlockSpec((1, LANES), lambda j: (0, j))
+    single = pl.BlockSpec((1, 1), lambda j: (0, 0))
+    results = pl.pallas_call(
+        gate,
+        grid=(blocks,),
+        out_shape=(
+            narrow,
+            narrow,
+            narrow,
+            narrow,
+            jax.ShapeDtypeStruct((rows, channels), jnp.float32),
+            jax.ShapeDtypeStruct((1, channels), jnp.float32),
+            jax.ShapeDtypeStruct((1, 1), jnp.float32),
+        ),
+        in_specs=[column] * 4
+        + [line, pl.BlockSpec((3, 1, rows, LANES), lambda j: (0, j, 0, 0)), line, single],
+        out_specs=[column] * 5 + [line, single],
+    )(
+        query_input, key_input, value_input, cotangent,
+        skip_gain.reshape(1, channels), flat, direct, rms,
     )
     return (*results[:5], results[5].reshape(channels), results[6].reshape(()))
 

time: 57.6 us -> 50.6 us (0.88)
  local copies, waits for them, and re-layouts: 9.19 us -> 0 us
  Pallas kernels: 45.7 us -> 49.8 us
  between operations: 2.41 us -> 0.64 us
    unnamed x6 -> x0, local copies, waits for them, and re-layouts: 9.19 us -> none
    pallas_call x0 -> x1, Pallas kernels: none -> 4.13 us  [fused_body(): pl.pallas_call(gate, grid=(blocks,), out_shape=(narrow, narrow, narrow, n...]
where the time goes in v2:
time: 50.6 us; the launch traced here: 50.4 us
  Pallas kernels  49.8 us (98%)
  between operations  0.64 us (1%)
    pallas_call x1, Pallas kernels, fused_body(): pl.pallas_call(functools.partial(kernel, devices, groups, count), out_sha...  45.7 us
    pallas_call x1, Pallas kernels, fused_body(): pl.pallas_call(gate, grid=(blocks,), out_shape=(narrow, narrow, narrow, n...  4.13 us

profile of v2, /device:TPU:0, one launch (start us, length us, event | category | flops | bytes accessed | tf_op | source)
XLA Modules:
  0.0 50.4 jit_solution(13042687928183093623)
XLA Ops:
  0.6 45.7 %shard_map.135 = (f32[3,4,128,128]{3,2,1,0:T(8,128)}, f32[1,512]{1,0:T(1,128)}, f32[1,1]{1,0:T(1,128)}) custom-call(bf16[128,512]{1,0:T(8,128)(2,1)} %q_ref.3, bf16[128,512]{1,0:T(8,128)(2,1)} %k_ref.3, bf16[128,512]{1,0:T(8,128)(2,1)} %v_ref.3, bf16[128,512]{1,0:T(8,128)(2,1)} %c_ref.3, f32[128,512]{1,0:T(8,128)} %h_ref.1, ...), custom_call_target="tpu_custom_call" | custom-call | tf_op jit(solution)/shard_map/pallas_call | solution.py:461
  46.3 4.1 %shard_map.136 = (bf16[128,512]{1,0:T(8,128)(2,1)}, bf16[128,512]{1,0:T(8,128)(2,1)}, bf16[128,512]{1,0:T(8,128)(2,1)}, bf16[128,512]{1,0:T(8,128)(2,1)}, f32[12...) custom-call(bf16[128,512]{1,0:T(8,128)(2,1)} %q_ref.3, bf16[128,512]{1,0:T(8,128)(2,1)} %k_ref.3, ...), custom_call_target="tpu_custom_call" | custom-call | tf_op jit(solution)/shard_map/pallas_call | solution.py:502
